TPU v7x, 128 devices: a whole 4x4x4 slice. The times are simulated.
128 devices in a mesh: dp: 32 (over y, x, z_hi), mp: 4 (over z_lo, core).
Axes of the slice: x: 4, y: 4, z: 4 (z_hi: 2, z_lo: 2; z = z_hi * 2 + z_lo), core: 2. Of those that a mesh axis runs over, the one named last changes fastest.
Arguments:
- page_pool: bfloat16 [2048, 128, 512], P('dp'), may hold values from -6 to 6
- move_count: int32 [32, 32], P('dp'), may hold values from 0 to 2, as said below
- send_slots: int32 [1024, 2], P('dp'), may hold values from 0 to 63, as said below
- page_table: int32 [2048, 16], P('dp'), may hold values from 0 to 127, as said below
- history_len: int32 [2048], P('dp'), may hold values from 1 to 2048, as said below
- queries: bfloat16 [2048, 8, 256], P('dp', 'mp'), may hold values from -6 to 6
- new_entry: bfloat16 [2048, 512], P('dp'), may hold values from -6 to 6
- residual: bfloat16 [2048, 2048], P('dp'), may hold values from -30 to 30
- out_proj: bfloat16 [2048, 2048], P('mp'), may hold values from -0.125 to 0.125
- ffn_gain: float32 [2048], replicated, may hold values from -0.5 to 0.5
- gate_proj: bfloat16 [2048, 16384], P(None, ('dp', 'mp')), may hold values from -0.125 to 0.125
- up_proj: bfloat16 [2048, 16384], P(None, ('dp', 'mp')), may hold values from -0.125 to 0.125
- down_proj: bfloat16 [16384, 2048], P(('dp', 'mp')), may hold values from -0.046875 to 0.046875
Outputs:
- arrived: bfloat16 [2048, 128, 512], P('dp')
- layer_out: bfloat16 [2048, 2048], P('dp')
Inputs may be any that keep to these rules, and one draw needn't show every extreme that they name: `move_count`: zero on the diagonal; in every draw one device receives exactly 2 pages from every other device. `send_slots`: only the first move_count[s, d] entries of row s * 32 + d are sent. `page_table`: for a game of device d, an entry e >= 64 equals 64 + s * 2 + c with c < move_count[s, d]. `history_len`: some game of some device reaches 2048 in every draw.
All inputs are finite; a program needn't handle non-finite values.
Results may differ from a plain program's by a relative error of at most 0.0075.
Values may be sent and summed in bfloat16 or wider, within the bound.
No kernel may reach another device: no remote copies, remote signals or barrier semaphores. Data moves between devices by JAX's collectives and lax.ppermute only.
A program may use at most 128 MiB of HBM per device.

v0:
```python
import math
import jax
import jax.numpy as jnp
from jax import lax
from jax.sharding import PartitionSpec as P


def copy_for_each(array, axis):
    peers = lax.axis_size(axis)
    return lax.all_to_all(
        jnp.broadcast_to(array[None], (peers, *array.shape)), axis, 0, 0, tiled=True
    )


def taken_together(array, axis):
    everything = copy_for_each(array, axis)
    return jnp.sum(everything, axis=0)


def in_blocks(array, dim, peers):
    lengths = array.shape
    tiles = array.reshape(*lengths[:dim], peers, lengths[dim] // peers, *lengths[dim + 1 :])
    return jnp.moveaxis(tiles, dim, 0)


def sum_at_owner(array, axis, dim):
    tiles = in_blocks(array, dim, lax.axis_size(axis))
    arrived = lax.all_to_all(tiles, axis, split_axis=0, concat_axis=0, tiled=True)
    return arrived.astype(jnp.float32).sum(axis=0)


def attend_block(query_blk, page_rows, length_blk, entry_blk):
    head_size = query_blk.shape[-1]
    keys = page_rows[:, :, :head_size]
    values = page_rows[:, :, head_size:]
    factor = 1.0 / math.sqrt(head_size)
    scores = (
        jnp.einsum("bhd,btd->bht", query_blk, keys, preferred_element_type=jnp.float32) * factor
    )
    own = (
        jnp.einsum(
            "bhd,bd->bh", query_blk, entry_blk[:, :head_size], preferred_element_type=jnp.float32
        )
        * factor
    )
    places = jnp.arange(page_rows.shape[1], dtype=jnp.int32)
    valid = places[None, None, :] < length_blk[:, None, None]
    scores = jnp.where(valid, scores, jnp.float32(-1e30))
    biggest = jnp.maximum(jnp.max(scores, axis=-1), own)
    probs = jnp.where(valid, jnp.exp(scores - biggest[..., None]), jnp.float32(0.0))
    prob_own = jnp.exp(own - biggest)
    denom = jnp.sum(probs, axis=-1) + prob_own
    weights = (probs / denom[..., None]).astype(jnp.bfloat16)
    weight_own = (prob_own / denom).astype(jnp.bfloat16)
    result = jnp.einsum("bht,btd->bhd", weights, values, preferred_element_type=jnp.float32)
    result = result + weight_own.astype(jnp.float32)[..., None] * entry_blk[
        :, None, head_size:
    ].astype(jnp.float32)
    return result.astype(jnp.bfloat16)


def local(
    page_pool,
    move_count,
    send_slots,
    page_table,
    history_len,
    queries,
    new_entry,
    residual,
    out_proj,
    ffn_gain,
    gate_proj,
    up_proj,
    down_proj,
):
    senders = lax.axis_size("dp")
    groups = lax.axis_size("mp")
    games = queries.shape[0]
    local_heads = queries.shape[1]
    head_size = queries.shape[2]
    page_len = page_pool.shape[1]
    width = page_pool.shape[2]
    slot_count = send_slots.shape[1]
    table_len = page_table.shape[1]
    live = jnp.arange(slot_count, dtype=jnp.int32)[None, :] < move_count[0][:, None]
    quarter = page_len // groups
    token_part = lax.dynamic_slice_in_dim(page_pool, lax.axis_index("mp") * quarter, quarter, 1)
    outgoing = token_part[send_slots]
    outgoing = jnp.where(live[:, :, None, None], outgoing, jnp.zeros((), jnp.bfloat16))
    partial_pages = lax.all_to_all(outgoing, "dp", split_axis=0, concat_axis=0, tiled=True)
    received = lax.all_gather(partial_pages, "mp", axis=2, tiled=True)
    arrived = received.reshape(senders * slot_count, page_len, width)
    every_page = jnp.concatenate([page_pool, arrived], axis=0)
    block = math.gcd(games, 8)
    table = page_table.reshape(-1, block, table_len)
    lengths = history_len.reshape(-1, block)
    query_dev = queries.reshape(-1, block, local_heads, head_size)
    entry_dev = new_entry.reshape(-1, block, width)

    def one_block(items):
        table_blk, length_blk, query_blk, entry_blk = items
        page_rows = every_page[table_blk].reshape(block, table_len * page_len, width)
        return attend_block(query_blk, page_rows, length_blk, entry_blk)

    attended = lax.map(one_block, (table, lengths, query_dev, entry_dev)).reshape(
        games, local_heads * head_size
    )
    head_part = jnp.dot(attended, out_proj, preferred_element_type=jnp.float32)
    stream_in = residual.astype(jnp.float32) + taken_together(head_part, "mp")
    scale_row = lax.rsqrt(jnp.mean(stream_in * stream_in, axis=-1, keepdims=True) + 1e-06)
    normed = (stream_in * scale_row * (1.0 + ffn_gain)).astype(jnp.bfloat16)
    piece = lax.all_gather(normed, "dp", axis=0, tiled=True)
    gate = jnp.dot(piece, gate_proj, preferred_element_type=jnp.float32)
    up_val = jnp.dot(piece, up_proj, preferred_element_type=jnp.float32)
    hidden = (jax.nn.gelu(gate, approximate=True) * up_val).astype(jnp.bfloat16)
    partial_out = sum_at_owner(
        jnp.dot(hidden, down_proj, preferred_element_type=jnp.float32).astype(jnp.bfloat16), "dp", 0
    )
    mixed = lax.psum(partial_out, "mp")
    layer_out = (stream_in + mixed).astype(jnp.bfloat16)
    return (arrived, layer_out)


def solution(mesh):
    in_specs = (
        P("dp", None, None),
        P("dp", None),
        P("dp", None),
        P("dp", None),
        P("dp"),
        P("dp", "mp", None),
        P("dp", None),
        P("dp", None),
        P("mp", None),
        P(),
        P(None, ("dp", "mp")),
        P(None, ("dp", "mp")),
        P(("dp", "mp"), None),
    )
    out_specs = (P("dp", None, None), P("dp", None))
    return jax.shard_map(local, mesh=mesh, in_specs=in_specs, out_specs=out_specs, check_vma=False)
```

profile of v0, /device:TPU:1, one launch (start us, length us, event | category | flops | bytes accessed | tf_op | source)
XLA Modules:
  0.0 678.5 jit_solution(8073125660301408105)
XLA Ops:
  7.2 0.8 compare_select_fusion.1
  8.3 0.7 iota_compare_fusion.1
  9.0 3.2 constant_dynamic-slice_fusion.1
  12.2 3.6 gather_fusion.1
  15.8 1.8 broadcast_select_fusion
  17.6 40.7 %all_to_all.15 = bf16[32,2,32,512]{3,2,1,0:T(8,128)(2,1)} all-to-all(bf16[32,2,32,512]{3,2,1,0:T(8,128)(2,1)S(1)} %broadcast_select_fusion), channel_id=1, replica_groups=mesh['dp'=32,'mp'=4] {'dp'}, dimensions={0} | all-to-all | bytes 4194304 | tf_op jit(solution)/shard_map/all_to_all | solution.py:91
  58.5 78.7 %all-gather.3.cloned.1.call-done = bf16[32,2,128,512]{3,2,1,0:T(8,128)(2,1)} async-done(((bf16[32,2,32,512]{3,2,1,0:T(8,128)(2,1)}), bf16[32,2,128,512]{3,2,1,0:T(8,128)(2,1)}) %all-gather.3.cloned.1.call-update) | async-done | bytes 8388624 | tf_op jit(solution)/shard_map/all_gather | solution.py:92
  137.2 13.8 %pad_maximum_fusion = bf16[128,128,512]{2,1,0:T(8,128)(2,1)} fusion(bf16[64,128,512]{2,1,0:T(8,128)(2,1)} %bitcast.59, bf16[64,128,512]{2,1,0:T(8,128)(2,1)} %param.15), kind=kLoop, calls=%fused_computation.35 | loop fusion | flops 8388608 | bytes 33554432 | tf_op jit(solution)/shard_map/concatenate | solution.py:94
  150.9 211.9 %while.10 = (s32[]{:T(128)}, bf16[8,8,2,256]{3,2,1,0:T(2,128)(2,1)S(1)}, s32[8,8]{1,0:T(8,128)S(1)}, bf16[8,8,2,256]{3,2,1,0:T(2,128)(2,1)}, s32[8,8,16]{2,1,0:T...) while((s32[]{:T(128)}, bf16[8,8,2,256]{3,2,1,0:T(2,128)(2,1)S(1)}, ...), condition=%wide.region_3.4_spmd, body=%wide.region_0.3_spmd.sunk | while | flops 33922544 | bytes 50886080 | solution.py:106
  151.0 14.1 %gather_fusion = bf16[128,128,512]{2,1,0:T(8,128)(2,1)} fusion(bf16[128,128,512]{2,1,0:T(8,128)(2,1)} %get-tuple-element.136, s32[1024]{0:T(1024)S(1)} %pad_clamp_fusion.3), kind=kCustom, calls=%fused_computation.clone.1 | custom fusion | bytes 33554944 | tf_op jit(solution)/shard_map/while/body/eval_jaxpr/gather | solution.py:103
  165.2 5.8 fusion.71
  170.9 0.7 dynamic-slice_bitcast_fusion.7
  171.7 0.8 fusion.69
  172.5 0.3 fusion.72
  172.8 4.6 fusion.74
  177.5 14.0 %gather_fusion = bf16[128,128,512]{2,1,0:T(8,128)(2,1)} fusion(bf16[128,128,512]{2,1,0:T(8,128)(2,1)} %get-tuple-element.136, s32[1024]{0:T(1024)S(1)} %pad_clamp_fusion.3), kind=kCustom, calls=%fused_computation.clone.1 | custom fusion | bytes 33554944 | tf_op jit(solution)/shard_map/while/body/eval_jaxpr/gather | solution.py:103
  191.7 5.8 fusion.71
  197.4 0.7 dynamic-slice_bitcast_fusion.7
  198.1 0.8 fusion.69
  199.3 4.6 fusion.74
  204.0 14.1 %gather_fusion = bf16[128,128,512]{2,1,0:T(8,128)(2,1)} fusion(bf16[128,128,512]{2,1,0:T(8,128)(2,1)} %get-tuple-element.136, s32[1024]{0:T(1024)S(1)} %pad_clamp_fusion.3), kind=kCustom, calls=%fused_computation.clone.1 | custom fusion | bytes 33554944 | tf_op jit(solution)/shard_map/while/body/eval_jaxpr/gather | solution.py:103
  218.2 5.8 fusion.71
  223.9 0.7 dynamic-slice_bitcast_fusion.7
  224.6 0.8 fusion.69
  225.8 4.6 fusion.74
  230.5 14.0 %gather_fusion = bf16[128,128,512]{2,1,0:T(8,128)(2,1)} fusion(bf16[128,128,512]{2,1,0:T(8,128)(2,1)} %get-tuple-element.136, s32[1024]{0:T(1024)S(1)} %pad_clamp_fusion.3), kind=kCustom, calls=%fused_computation.clone.1 | custom fusion | bytes 33554944 | tf_op jit(solution)/shard_map/while/body/eval_jaxpr/gather | solution.py:103
  244.7 5.8 fusion.71
  250.4 0.7 dynamic-slice_bitcast_fusion.7
  251.1 0.8 fusion.69
  252.2 4.6 fusion.74
  257.0 14.1 %gather_fusion = bf16[128,128,512]{2,1,0:T(8,128)(2,1)} fusion(bf16[128,128,512]{2,1,0:T(8,128)(2,1)} %get-tuple-element.136, s32[1024]{0:T(1024)S(1)} %pad_clamp_fusion.3), kind=kCustom, calls=%fused_computation.clone.1 | custom fusion | bytes 33554944 | tf_op jit(solution)/shard_map/while/body/eval_jaxpr/gather | solution.py:103
  271.1 5.8 fusion.71
  276.9 0.7 dynamic-slice_bitcast_fusion.7
  277.6 0.8 fusion.69
  278.7 4.6 fusion.74
  283.5 14.1 %gather_fusion = bf16[128,128,512]{2,1,0:T(8,128)(2,1)} fusion(bf16[128,128,512]{2,1,0:T(8,128)(2,1)} %get-tuple-element.136, s32[1024]{0:T(1024)S(1)} %pad_clamp_fusion.3), kind=kCustom, calls=%fused_computation.clone.1 | custom fusion | bytes 33554944 | tf_op jit(solution)/shard_map/while/body/eval_jaxpr/gather | solution.py:103
  297.6 5.8 fusion.71
  303.4 0.7 dynamic-slice_bitcast_fusion.7
  304.1 0.8 fusion.69
  305.2 4.6 fusion.74
  310.0 14.0 %gather_fusion = bf16[128,128,512]{2,1,0:T(8,128)(2,1)} fusion(bf16[128,128,512]{2,1,0:T(8,128)(2,1)} %get-tuple-element.136, s32[1024]{0:T(1024)S(1)} %pad_clamp_fusion.3), kind=kCustom, calls=%fused_computation.clone.1 | custom fusion | bytes 33554944 | tf_op jit(solution)/shard_map/while/body/eval_jaxpr/gather | solution.py:103
  324.1 5.8 fusion.71
  329.9 0.7 dynamic-slice_bitcast_fusion.7
  330.6 0.8 fusion.69
  331.7 4.6 fusion.74
  336.5 14.1 %gather_fusion = bf16[128,128,512]{2,1,0:T(8,128)(2,1)} fusion(bf16[128,128,512]{2,1,0:T(8,128)(2,1)} %get-tuple-element.136, s32[1024]{0:T(1024)S(1)} %pad_clamp_fusion.3), kind=kCustom, calls=%fused_computation.clone.1 | custom fusion | bytes 33554944 | tf_op jit(solution)/shard_map/while/body/eval_jaxpr/gather | solution.py:103
  350.6 5.8 fusion.71
  356.4 0.7 dynamic-slice_bitcast_fusion.7
  357.1 0.8 fusion.69
  358.2 4.6 fusion.74
  362.9 0.5 fusion.50
  363.4 1.6 broadcast_in_dim.61
  365.0 4.4 all-to-all-start.1
  369.5 23.6 %all-to-all-done.1 = f32[4,64,2048]{2,1,0:T(8,128)} async-done(((f32[4,64,2048]{2,1,0:T(8,128)}), f32[4,64,2048]{2,1,0:T(8,128)}, u32[]{:S(2)}, u32[]{:S(2)}) %all-to-all-start.1) | async-done | bytes 2097184 | tf_op jit(solution)/shard_map/all_to_all | solution.py:10
  393.0 1.8 reduce_sum.36
  395.0 0.8 multiply_convert_fusion
  395.9 105.4 %all-gather.5.cloned.1.call-done = bf16[2048,2048]{1,0:T(8,128)(2,1)} async-done(((bf16[64,2048]{1,0:T(8,128)(2,1)}), bf16[2048,2048]{1,0:T(8,128)(2,1)}) %all-gather.5.cloned.1.call-update) | async-done | bytes 8388624 | tf_op jit(solution)/shard_map/all_gather | solution.py:113
  501.3 6.8 %fusion.51 = f32[2048,128]{1,0:T(8,128)} fusion(bf16[2048,2048]{1,0:T(8,128)(2,1)} %all-gather.5.cloned.1.call-done, bf16[2048,128]{1,0:T(8,128)(2,1)} %param.25), kind=kOutput, calls=%fused_computation.69 | convolution fusion | flops 1073741824 | bytes 9961472 | tf_op jit(solution)/shard_map/dot_general | solution.py:114
  508.1 13.2 %convolution_convert_fusion = bf16[2048,2048]{1,0:T(8,128)(2,1)} fusion(bf16[128,2048]{1,0:T(8,128)(2,1)S(1)} %copy-done.2, bf16[2048,2048]{1,0:T(8,128)(2,1)} %all-gather.5.cloned.1.call-done, bf16[2048,128]{1,0:T(8,128)(2,1)} %param.26, f32[2048,128]{1,0:T(8,128)} %fusion.51), kind=kOutput, calls=%fused_computation.37 | convolution fusion | flops 2154299392 | bytes 18874368 | tf_op jit(solution)/shard_map/dot_general | solution.py:118
  521.3 102.2 %all_to_all.16 = bf16[32,64,2048]{2,1,0:T(8,128)(2,1)S(1)} all-to-all(bf16[32,64,2048]{2,1,0:T(8,128)(2,1)} %bitcast.58), channel_id=1, replica_groups=mesh['dp'=32,'mp'=4] {'dp'}, dimensions={0} | all-to-all | bytes 16777216 | tf_op jit(solution)/shard_map/all_to_all | solution.py:28
  623.5 2.9 convert_reduce_fusion
  626.5 35.9 %all-reduce.2.cloned.1.call-done = f32[64,2048]{1,0:T(8,128)} async-done(((f32[64,2048]{1,0:T(8,128)}), f32[64,2048]{1,0:T(8,128)}) %all-reduce.2.cloned.1.call-update) | async-done | bytes 524304 | tf_op jit(solution)/shard_map/psum | solution.py:120
  662.4 1.8 add_convert_fusion
  664.2 7.8 %copy.39 = bf16[64,128,512]{2,1,0:T(8,128)(2,1)} copy(bf16[64,128,512]{2,1,0:T(8,128)(2,1)} %bitcast.60) | data formatting | bytes 16777216
  (99 shorter events, 4.4 us)
Async XLA Ops:
  7.2 355.8 %copy-start = (bf16[512,2048]{1,0:T(8,128)(2,1)S(1)}, bf16[512,2048]{1,0:T(8,128)(2,1)}, u32[]{:S(2)}) copy-start(bf16[512,2048]{1,0:T(8,128)(2,1)} %param.23) | copy-start | bytes 6291460
  7.2 130.0 %all-gather.3.cloned.1.call-start = ((), (), s32[]{:S(2)}) async-start(), calls=%async_computation.3 | async-start | bytes 10485760 | tf_op jit(solution)/shard_map/all_gather | solution.py:92
  12.2 46.1 %copy-start.3 = (s32[64,16]{0,1:T(8,128)S(1)}, s32[64,16]{0,1:T(8,128)}, u32[]{:S(2)}) copy-start(s32[64,16]{0,1:T(8,128)} %param.18) | copy-start | bytes 12292
  12.2 46.2 %copy-start.5 = (s32[64]{0:T(128)S(1)}, s32[64]{0:T(128)}, u32[]{:S(2)}) copy-start(s32[64]{0:T(128)} %param.19) | copy-start | bytes 772
  362.9 6.6 copy-start.4
  362.9 31.9 %copy-start.1 = (bf16[64,2048]{1,0:T(8,128)(2,1)S(1)}, bf16[64,2048]{1,0:T(8,128)(2,1)}, u32[]{:S(2)}) copy-start(bf16[64,2048]{1,0:T(8,128)(2,1)} %param.22) | copy-start | bytes 786436
  365.0 28.1 %all-to-all-start.1 = ((f32[4,64,2048]{2,1,0:T(8,128)}), f32[4,64,2048]{2,1,0:T(8,128)}, u32[]{:S(2)}, u32[]{:S(2)}) async-start(f32[4,64,2048]{2,1,0:T(8,128)} %broadcast_in_dim.61), calls=%async_computation.1 | async-start | bytes 4194304 | tf_op jit(solution)/shard_map/all_to_all | solution.py:10
  369.4 138.7 %copy-start.2 = (bf16[128,2048]{1,0:T(8,128)(2,1)S(1)}, bf16[128,2048]{1,0:T(8,128)(2,1)}, u32[]{:S(2)}) copy-start(bf16[128,2048]{1,0:T(8,128)(2,1)} %param.27) | copy-start | bytes 1572868
  369.4 131.9 %all-gather.5.cloned.1.call-start = ((), (), s32[]{:S(2)}) async-start(), calls=%async_computation.4 | async-start | bytes 8650752 | tf_op jit(solution)/shard_map/all_gather | solution.py:113
  395.9 266.6 %all-reduce.2.cloned.1.call-start = ((), (), s32[]{:S(2)}) async-start(), calls=%async_computation.5 | async-start | bytes 1048576 | tf_op jit(solution)/shard_map/psum | solution.py:120
Sparse Core Ops, SparseCore 0:
  58.4 78.7 all-gather.2
  396.0 105.2 all-gather.4
  626.6 35.7 all-reduce.1
where the time goes:
time: 681 us; the launch traced here: 679 us
  waiting for transfers between devices  244 us (36%)
  blocking collectives  143 us (21%)
  local copies, waits for them, and re-layouts  135 us (20%)
  matrix products  110 us (16%)
  other arithmetic  27.9 us (4%)
  between operations  13.9 us (2%)
    gather x8, local copies, waits for them, and re-layouts, one_block(): every_page[table_blk].reshape(block, table_len * page_len, width)  112 us
    all_gather x1, waiting for transfers between devices, local(): piece = lax.all_gather(normed, 'dp', axis=0, tiled=True)  105 us
    all_to_all x1, blocking collectives, sum_at_owner(): lax.all_to_all(tiles, axis, split_axis=0, concat_axis=0, tiled=True)  102 us
    all_gather x1, waiting for transfers between devices, local(): received = lax.all_gather(partial_pages, 'mp', axis=2, tiled=True)  78.7 us
    dot_general x8, matrix products, attend_block(): jnp.einsum('bhd,btd->bht', query_blk, keys, preferred_element_type=jnp.fl...  46 us
    all_to_all x1, blocking collectives, local(): lax.all_to_all(outgoing, 'dp', split_axis=0, concat_axis=0, tiled=True)  40.7 us
    dot_general x8, matrix products, attend_block(): jnp.einsum('bht,btd->bhd', weights, values, preferred_element_type=jnp.fl...  37.1 us
    psum x1, waiting for transfers between devices, local(): mixed = lax.psum(partial_out, 'mp')  35.9 us
  transfers between devices with their start and end apart: 4, of which 4 were waited for; matrix products, arithmetic and copies ran while one was open for 0% of the time, Pallas kernels for 0%

commit v1 on v0

--- a/solution.py
+++ b/solution.py
@@ -89,7 +89,10 @@
     outgoing = token_part[send_slots]
     outgoing = jnp.where(live[:, :, None, None], outgoing, jnp.zeros((), jnp.bfloat16))
     partial_pages = lax.all_to_all(outgoing, "dp", split_axis=0, concat_axis=0, tiled=True)
-    received = lax.all_gather(partial_pages, "mp", axis=2, tiled=True)
+    peers_2 = lax.axis_size("mp")
+    parts = jnp.stack([partial_pages for _ in range(peers_2)])
+    parts = lax.all_to_all(parts, "mp", split_axis=0, concat_axis=0)
+    received = jnp.concatenate(parts, axis=2)
     arrived = received.reshape(senders * slot_count, page_len, width)
     every_page = jnp.concatenate([page_pool, arrived], axis=0)
     block = math.gcd(games, 8)

time: 681 us -> 703 us (1.032)
  starting transfers between devices: 4.55 us -> 13.3 us
  waiting for transfers between devices: 244 us -> 252 us
    all_to_all x0 -> x1, waiting for transfers between devices: none -> 92.1 us  [local(): parts = lax.all_to_all(parts, 'mp', split_axis=0, concat_axis=0)]
    all_gather x1 -> x0, waiting for transfers between devices: 78.7 us -> none  [local(): received = lax.all_gather(partial_pages, 'mp', axis=2, tiled=True)]
    all_to_all x0 -> x1, local copies, waits for them, and re-layouts: none -> 8.44 us  [local(): parts = lax.all_to_all(parts, 'mp', split_axis=0, concat_axis=0)]
    unnamed x15 -> x14, local copies, waits for them, and re-layouts: 7.9 us -> 0.12 us
    all_to_all x0 -> x1, starting transfers between devices: none -> 7.67 us  [local(): parts = lax.all_to_all(parts, 'mp', split_axis=0, concat_axis=0)]
where the time goes in v1:
time: 703 us; the launch traced here: 701 us
  waiting for transfers between devices  252 us (36%)
  blocking collectives  143 us (20%)
  local copies, waits for them, and re-layouts  140 us (20%)
  matrix products  110 us (16%)
  other arithmetic  27.9 us (4%)
  between operations  14.1 us (2%)
  starting transfers between devices  13.3 us (2%)
    gather x8, local copies, waits for them, and re-layouts, one_block(): every_page[table_blk].reshape(block, table_len * page_len, width)  112 us
    all_to_all x1, blocking collectives, sum_at_owner(): lax.all_to_all(tiles, axis, split_axis=0, concat_axis=0, tiled=True)  102 us
    all_gather x1, waiting for transfers between devices, local(): piece = lax.all_gather(normed, 'dp', axis=0, tiled=True)  99.4 us
    all_to_all x1, waiting for transfers between devices, local(): parts = lax.all_to_all(parts, 'mp', split_axis=0, concat_axis=0)  92.1 us
    dot_general x8, matrix products, attend_block(): jnp.einsum('bhd,btd->bht', query_blk, keys, preferred_element_type=jnp.fl...  46 us
    all_to_all x1, blocking collectives, local(): lax.all_to_all(outgoing, 'dp', split_axis=0, concat_axis=0, tiled=True)  40.6 us
    dot_general x8, matrix products, attend_block(): jnp.einsum('bht,btd->bhd', weights, values, preferred_element_type=jnp.fl...  37.1 us
    psum x1, waiting for transfers between devices, local(): mixed = lax.psum(partial_out, 'mp')  36 us
  transfers between devices with their start and end apart: 4, of which 4 were waited for; matrix products, arithmetic and copies ran while one was open for 0% of the time, Pallas kernels for 0%

profile of v1, /device:TPU:1, one launch (start us, length us, event | category | flops | bytes accessed | tf_op | source)
XLA Modules:
  0.0 700.9 jit_solution(6940298757696859963)
XLA Ops:
  7.2 0.8 compare_select_fusion.1
  8.2 0.7 iota_compare_fusion.1
  9.0 3.2 constant_dynamic-slice_fusion.1
  12.1 3.6 gather_fusion.1
  15.7 1.8 broadcast_select_fusion
  17.5 40.6 %all_to_all.20 = bf16[32,2,32,512]{3,2,1,0:T(8,128)(2,1)S(1)} all-to-all(bf16[32,2,32,512]{3,2,1,0:T(8,128)(2,1)S(1)} %broadcast_select_fusion), channel_id=1, replica_groups=mesh['dp'=32,'mp'=4] {'dp'}, dimensions={0} | all-to-all | bytes 4194304 | tf_op jit(solution)/shard_map/all_to_all | solution.py:91
  58.1 4.5 stack.2
  62.6 7.7 %all-to-all-start.1 = ((bf16[4,32,2,32,512]{4,3,2,1,0:T(8,128)(2,1)}), bf16[4,32,2,32,512]{4,3,2,1,0:T(8,128)(2,1)}, u32[]{:S(2)}, u32[]{:S(2)}) async-start(bf16[4,32,2,32,512]{4,3,2,1,0:T(8,128)(2,1)} %stack.2), calls=%async_computation.1 | async-start | bytes 16777216 | tf_op jit(solution)/shard_map/all_to_all | solution.py:94
  70.4 92.1 %all-to-all-done.1 = bf16[4,32,2,32,512]{4,3,2,1,0:T(8,128)(2,1)} async-done(((bf16[4,32,2,32,512]{4,3,2,1,0:T(8,128)(2,1)}), bf16[4,32,2,32,512]{4,3,2,1,0:T(8,128)(2,1)}, u32[]{:S(2)}, u32[]{:S(2)}) %all-to-all-start.1) | async-done | bytes 8388640 | tf_op jit(solution)/shard_map/all_to_all | solution.py:94
  162.4 8.4 %copy.25 = bf16[4,32,2,32,512]{4,3,0,2,1:T(8,128)(2,1)} copy(bf16[4,32,2,32,512]{4,3,2,1,0:T(8,128)(2,1)} %all-to-all-done.1) | data formatting | bytes 16777216 | tf_op jit(solution)/shard_map/all_to_all | solution.py:94
  170.9 13.8 %pad_maximum_fusion = bf16[128,128,512]{2,1,0:T(8,128)(2,1)} fusion(bf16[64,128,512]{2,1,0:T(8,128)(2,1)} %bitcast.61, bf16[64,128,512]{2,1,0:T(8,128)(2,1)} %param.15), kind=kLoop, calls=%fused_computation.35 | loop fusion | flops 8388608 | bytes 33554432 | tf_op jit(solution)/shard_map/concatenate | solution.py:97
  184.7 211.9 %while.10 = (s32[]{:T(128)}, bf16[8,8,2,256]{3,2,1,0:T(2,128)(2,1)S(1)}, s32[8,8]{1,0:T(8,128)S(1)}, bf16[8,8,2,256]{3,2,1,0:T(2,128)(2,1)}, s32[8,8,16]{2,1,0:T...) while((s32[]{:T(128)}, bf16[8,8,2,256]{3,2,1,0:T(2,128)(2,1)S(1)}, ...), condition=%wide.region_3.4_spmd, body=%wide.region_0.3_spmd.sunk | while | flops 33922544 | bytes 50886080 | solution.py:109
  184.8 14.1 %gather_fusion = bf16[128,128,512]{2,1,0:T(8,128)(2,1)} fusion(bf16[128,128,512]{2,1,0:T(8,128)(2,1)} %get-tuple-element.136, s32[1024]{0:T(1024)S(1)} %pad_clamp_fusion.3), kind=kCustom, calls=%fused_computation.clone.1 | custom fusion | bytes 33554944 | tf_op jit(solution)/shard_map/while/body/eval_jaxpr/gather | solution.py:106
  198.9 5.8 fusion.71
  204.7 0.7 dynamic-slice_bitcast_fusion.7
  205.4 0.8 fusion.69
  206.5 4.6 fusion.74
  211.3 14.0 %gather_fusion = bf16[128,128,512]{2,1,0:T(8,128)(2,1)} fusion(bf16[128,128,512]{2,1,0:T(8,128)(2,1)} %get-tuple-element.136, s32[1024]{0:T(1024)S(1)} %pad_clamp_fusion.3), kind=kCustom, calls=%fused_computation.clone.1 | custom fusion | bytes 33554944 | tf_op jit(solution)/shard_map/while/body/eval_jaxpr/gather | solution.py:106
  225.4 5.8 fusion.71
  231.2 0.7 dynamic-slice_bitcast_fusion.7
  231.9 0.8 fusion.69
  233.0 4.6 fusion.74
  237.7 14.1 %gather_fusion = bf16[128,128,512]{2,1,0:T(8,128)(2,1)} fusion(bf16[128,128,512]{2,1,0:T(8,128)(2,1)} %get-tuple-element.136, s32[1024]{0:T(1024)S(1)} %pad_clamp_fusion.3), kind=kCustom, calls=%fused_computation.clone.1 | custom fusion | bytes 33554944 | tf_op jit(solution)/shard_map/while/body/eval_jaxpr/gather | solution.py:106
  251.9 5.8 fusion.71
  257.7 0.7 dynamic-slice_bitcast_fusion.7
  258.4 0.8 fusion.69
  259.5 4.6 fusion.74
  264.2 14.0 %gather_fusion = bf16[128,128,512]{2,1,0:T(8,128)(2,1)} fusion(bf16[128,128,512]{2,1,0:T(8,128)(2,1)} %get-tuple-element.136, s32[1024]{0:T(1024)S(1)} %pad_clamp_fusion.3), kind=kCustom, calls=%fused_computation.clone.1 | custom fusion | bytes 33554944 | tf_op jit(solution)/shard_map/while/body/eval_jaxpr/gather | solution.py:106
  278.4 5.8 fusion.71
  284.1 0.7 dynamic-slice_bitcast_fusion.7
  284.9 0.8 fusion.69
  286.0 4.6 fusion.74
  290.7 14.1 %gather_fusion = bf16[128,128,512]{2,1,0:T(8,128)(2,1)} fusion(bf16[128,128,512]{2,1,0:T(8,128)(2,1)} %get-tuple-element.136, s32[1024]{0:T(1024)S(1)} %pad_clamp_fusion.3), kind=kCustom, calls=%fused_computation.clone.1 | custom fusion | bytes 33554944 | tf_op jit(solution)/shard_map/while/body/eval_jaxpr/gather | solution.py:106
  304.9 5.8 fusion.71
  310.6 0.7 dynamic-slice_bitcast_fusion.7
  311.3 0.8 fusion.69
  312.5 4.6 fusion.74
  317.2 14.1 %gather_fusion = bf16[128,128,512]{2,1,0:T(8,128)(2,1)} fusion(bf16[128,128,512]{2,1,0:T(8,128)(2,1)} %get-tuple-element.136, s32[1024]{0:T(1024)S(1)} %pad_clamp_fusion.3), kind=kCustom, calls=%fused_computation.clone.1 | custom fusion | bytes 33554944 | tf_op jit(solution)/shard_map/while/body/eval_jaxpr/gather | solution.py:106
  331.4 5.8 fusion.71
  337.1 0.7 dynamic-slice_bitcast_fusion.7
  337.8 0.8 fusion.69
  339.0 4.6 fusion.74
  343.7 14.0 %gather_fusion = bf16[128,128,512]{2,1,0:T(8,128)(2,1)} fusion(bf16[128,128,512]{2,1,0:T(8,128)(2,1)} %get-tuple-element.136, s32[1024]{0:T(1024)S(1)} %pad_clamp_fusion.3), kind=kCustom, calls=%fused_computation.clone.1 | custom fusion | bytes 33554944 | tf_op jit(solution)/shard_map/while/body/eval_jaxpr/gather | solution.py:106
  357.9 5.8 fusion.71
  363.6 0.7 dynamic-slice_bitcast_fusion.7
  364.3 0.8 fusion.69
  365.5 4.6 fusion.74
  370.2 14.1 %gather_fusion = bf16[128,128,512]{2,1,0:T(8,128)(2,1)} fusion(bf16[128,128,512]{2,1,0:T(8,128)(2,1)} %get-tuple-element.136, s32[1024]{0:T(1024)S(1)} %pad_clamp_fusion.3), kind=kCustom, calls=%fused_computation.clone.1 | custom fusion | bytes 33554944 | tf_op jit(solution)/shard_map/while/body/eval_jaxpr/gather | solution.py:106
  384.4 5.8 fusion.71
  390.1 0.7 dynamic-slice_bitcast_fusion.7
  390.8 0.8 fusion.69
  392.0 4.6 fusion.74
  397.1 1.5 broadcast_in_dim.61
  398.7 5.4 all-to-all-start.2
  404.1 24.8 %all-to-all-done.2 = f32[4,64,2048]{2,1,0:T(8,128)} async-done(((f32[4,64,2048]{2,1,0:T(8,128)}), f32[4,64,2048]{2,1,0:T(8,128)}, u32[]{:S(2)}, u32[]{:S(2)}) %all-to-all-start.2) | async-done | bytes 2097184 | tf_op jit(solution)/shard_map/all_to_all | solution.py:10
  428.9 1.8 reduce_sum.36
  430.8 0.8 multiply_convert_fusion
  431.9 99.4 %all-gather.2.cloned.1.call-done = bf16[2048,2048]{1,0:T(8,128)(2,1)} async-done(((bf16[64,2048]{1,0:T(8,128)(2,1)}), bf16[2048,2048]{1,0:T(8,128)(2,1)}) %all-gather.2.cloned.1.call-update) | async-done | bytes 8388624 | tf_op jit(solution)/shard_map/all_gather | solution.py:116
  531.3 6.8 fusion.51
  538.1 13.1 %convolution_convert_fusion = bf16[2048,2048]{1,0:T(8,128)(2,1)} fusion(bf16[128,2048]{1,0:T(8,128)(2,1)S(1)} %copy-done.2, bf16[2048,2048]{1,0:T(8,128)(2,1)} %all-gather.2.cloned.1.call-done, bf16[2048,128]{1,0:T(8,128)(2,1)} %param.26, f32[2048,128]{1,0:T(8,128)} %fusion.51), kind=kOutput, calls=%fused_computation.37 | convolution fusion | flops 2154299392 | bytes 18874368 | tf_op jit(solution)/shard_map/dot_general | solution.py:121
  551.2 102.2 %all_to_all.21 = bf16[32,64,2048]{2,1,0:T(8,128)(2,1)S(1)} all-to-all(bf16[32,64,2048]{2,1,0:T(8,128)(2,1)} %bitcast.60), channel_id=1, replica_groups=mesh['dp'=32,'mp'=4] {'dp'}, dimensions={0} | all-to-all | bytes 16777216 | tf_op jit(solution)/shard_map/all_to_all | solution.py:28
  653.3 3.0 convert_reduce_fusion
  656.3 36.0 %all-reduce.2.cloned.1.call-done = f32[64,2048]{1,0:T(8,128)} async-done(((f32[64,2048]{1,0:T(8,128)}), f32[64,2048]{1,0:T(8,128)}) %all-reduce.2.cloned.1.call-update) | async-done | bytes 524304 | tf_op jit(solution)/shard_map/psum | solution.py:123
  692.3 1.8 add_convert_fusion
  (99 shorter events, 5.3 us)
Async XLA Ops:
  7.2 389.5 %copy-start = (bf16[512,2048]{1,0:T(8,128)(2,1)S(1)}, bf16[512,2048]{1,0:T(8,128)(2,1)}, u32[]{:S(2)}) copy-start(bf16[512,2048]{1,0:T(8,128)(2,1)} %param.23) | copy-start | bytes 6291460
  62.6 7.7 %copy-start.3 = (s32[64,16]{0,1:T(8,128)S(1)}, s32[64,16]{0,1:T(8,128)}, u32[]{:S(2)}) copy-start(s32[64,16]{0,1:T(8,128)} %param.18) | copy-start | bytes 12292
  62.6 7.8 %copy-start.5 = (s32[64]{0:T(128)S(1)}, s32[64]{0:T(128)}, u32[]{:S(2)}) copy-start(s32[64]{0:T(128)} %param.19) | copy-start | bytes 772
  62.6 99.9 %all-to-all-start.1 = ((bf16[4,32,2,32,512]{4,3,2,1,0:T(8,128)(2,1)}), bf16[4,32,2,32,512]{4,3,2,1,0:T(8,128)(2,1)}, u32[]{:S(2)}, u32[]{:S(2)}) async-start(bf16[4,32,2,32,512]{4,3,2,1,0:T(8,128)(2,1)} %stack.2), calls=%async_computation.1 | async-start | bytes 16777216 | tf_op jit(solution)/shard_map/all_to_all | solution.py:94
  396.6 7.5 %copy-start.4 = (f32[2048]{0:T(1024)S(1)}, f32[2048]{0:T(1024)}, u32[]{:S(2)}) copy-start(f32[2048]{0:T(1024)} %param.24) | copy-start | bytes 24580
  396.6 34.0 %copy-start.1 = (bf16[64,2048]{1,0:T(8,128)(2,1)S(1)}, bf16[64,2048]{1,0:T(8,128)(2,1)}, u32[]{:S(2)}) copy-start(bf16[64,2048]{1,0:T(8,128)(2,1)} %param.22) | copy-start | bytes 786436
  398.7 30.2 %all-to-all-start.2 = ((f32[4,64,2048]{2,1,0:T(8,128)}), f32[4,64,2048]{2,1,0:T(8,128)}, u32[]{:S(2)}, u32[]{:S(2)}) async-start(f32[4,64,2048]{2,1,0:T(8,128)} %broadcast_in_dim.61), calls=%async_computation.2 | async-start | bytes 4194304 | tf_op jit(solution)/shard_map/all_to_all | solution.py:10
  404.1 134.0 %copy-start.2 = (bf16[128,2048]{1,0:T(8,128)(2,1)S(1)}, bf16[128,2048]{1,0:T(8,128)(2,1)}, u32[]{:S(2)}) copy-start(bf16[128,2048]{1,0:T(8,128)(2,1)} %param.27) | copy-start | bytes 1572868
  404.1 127.2 %all-gather.2.cloned.1.call-start = ((), (), s32[]{:S(2)}) async-start(), calls=%async_computation.4 | async-start | bytes 8650752 | tf_op jit(solution)/shard_map/all_gather | solution.py:116
  431.7 260.6 %all-reduce.2.cloned.1.call-start = ((), (), s32[]{:S(2)}) async-start(), calls=%async_computation.5 | async-start | bytes 1048576 | tf_op jit(solution)/shard_map/psum | solution.py:123
Sparse Core Ops, SparseCore 0:
  431.8 99.4 all-gather.1
  656.4 35.8 all-reduce.1
